TPU v7x, 256 devices: a whole 4x4x8 slice. The times are simulated.
256 devices in a mesh: expert: 8 (over x, z_lo), shard: 32 (over z_hi, y, core).
Axes of the slice: x: 4, y: 4, z: 8 (z_hi: 4, z_lo: 2; z = z_hi * 2 + z_lo), core: 2. Of those that a mesh axis runs over, the one named last changes fastest.
Arguments:
- tokens: bfloat16 [2048, 4096], P(('expert', 'shard')), may hold values from -6 to 6
- expert_ids: int32 [2048, 2], P(('expert', 'shard')), may hold values from 0 to 7, all different within a row; in each aligned block of 8 rows (0 to 7, 8 to 15, ...) at most 4 rows name the same one
- route_weights: float32 [2048, 2], P(('expert', 'shard')), may hold values from 0.1 to 1
- w_gate: bfloat16 [8, 4096, 12288], P('expert', None, 'shard'), may hold values from -0.09375 to 0.09375
- w_up: bfloat16 [8, 4096, 12288], P('expert', None, 'shard'), may hold values from -0.09375 to 0.09375
- w_down: bfloat16 [8, 12288, 4096], P('expert', 'shard'), may hold values from -0.0546875 to 0.0546875
Outputs:
- combined: bfloat16 [2048, 4096], P(('expert', 'shard'))
Inputs may be any that keep to these rules, and one draw needn't show every extreme that they name: `expert_ids`: each row names 2 different experts. Among the rows of one device no expert is named by more than 4 rows, a bound that some block reaches on some devices.
All inputs are finite; a program needn't handle non-finite values.
Results may differ from a plain program's by a relative error of at most 0.015.
Values may be sent and summed in bfloat16 or wider, within the bound.
A program may use at most 128 MiB of HBM per device.

v0:
```python
import jax
import jax.numpy as jnp
from jax import lax
from jax.sharding import PartitionSpec as P


def slot_matches(block_ids, groups, capacity):
    block_size, top_count = block_ids.shape
    flat_ids = block_ids.reshape(block_size * top_count)
    expert_iota = jnp.arange(groups, dtype=jnp.int32)
    member = (flat_ids[:, None] == expert_iota[None, :]).astype(jnp.int32)
    before = jnp.cumsum(member, axis=0) - member
    position = jnp.sum(before * member, axis=1)
    slot_ids = (flat_ids * capacity + position).reshape(block_size, top_count)
    slot_iota = jnp.arange(groups * capacity, dtype=jnp.int32)
    return slot_ids[:, :, None] == slot_iota[None, None, :]


def shards(tokens, expert_ids, route_weights, w_gate, w_up, w_down):
    experts = lax.axis_size("expert")
    block_size, model_width = tokens.shape
    top_count = expert_ids.shape[1]
    capacity = min(block_size, 2 * block_size * top_count // experts)
    gate_local = w_gate[0]
    up_local = w_up[0]
    down_local = w_down[0]
    local_matches = slot_matches(expert_ids, experts, capacity)
    own_table = jnp.sum(jnp.where(local_matches, route_weights[:, :, None], 0.0), axis=1)
    picker = jnp.sum(local_matches.astype(jnp.float32), axis=1).astype(jnp.bfloat16)
    outgoing = jnp.einsum("tj,td->jd", picker, tokens, preferred_element_type=jnp.float32)
    outgoing = outgoing.astype(jnp.bfloat16).reshape(experts, capacity, model_width)
    arrived = lax.all_to_all(outgoing, "expert", split_axis=0, concat_axis=0, tiled=True)
    row_block = lax.all_gather(arrived[None], "shard", axis=0, tiled=True)
    row_shape = row_block.shape
    flat_rows = row_block.reshape(-1, row_shape[-1])
    gate_proj = jnp.dot(flat_rows, gate_local, preferred_element_type=jnp.float32)
    up_proj = jnp.dot(flat_rows, up_local, preferred_element_type=jnp.float32)
    hidden = (jax.nn.silu(gate_proj) * up_proj).astype(jnp.bfloat16)
    result = jnp.dot(hidden, down_local, preferred_element_type=jnp.float32)
    partials = result.astype(jnp.bfloat16).reshape(row_shape)
    terms = lax.optimization_barrier(partials).astype(jnp.float32)
    summed = lax.psum_scatter(
        terms.astype(jnp.bfloat16), "shard", scatter_dimension=0, tiled=True
    ).astype(jnp.float32)
    returned = lax.all_to_all(
        summed.astype(jnp.bfloat16), "expert", split_axis=1, concat_axis=1, tiled=True
    ).astype(summed.dtype)
    returned = returned.reshape(experts * capacity, model_width)
    combined = jnp.dot(own_table, returned)
    return combined.astype(jnp.bfloat16)


def solution(mesh):
    placed = (
        P(("expert", "shard"), None),
        P(("expert", "shard"), None),
        P(("expert", "shard"), None),
        P("expert", None, "shard"),
        P("expert", None, "shard"),
        P("expert", "shard", None),
    )
    return jax.shard_map(
        shards, mesh=mesh, in_specs=placed, out_specs=P(("expert", "shard"), None), check_vma=False
    )
```

profile of v0, /device:TPU:24, one launch (start us, length us, event | category | flops | bytes accessed | tf_op | source)
XLA Modules:
  0.0 302.7 jit_solution(13382335335891866292)
XLA Ops:
  6.5 0.0 copy-start
  6.5 0.0 all-gather.3.cloned.1.call-start
  6.5 0.9 copy.18
  7.4 0.1 eq.28
  7.5 0.1 fusion.7
  7.6 0.2 select_reduce_fusion.1
  7.8 0.1 reduce_sum.30
  7.9 0.1 copy.20
  8.0 0.8 convert_reduce_fusion
  8.8 1.1 convolution_convert_fusion.1
  9.9 0.8 reshape.21
  10.7 13.0 %all_to_all.10 = bf16[8,4,4096]{2,1,0:T(4,128)(2,1)} all-to-all(bf16[8,4,4096]{2,1,0:T(4,128)(2,1)} %reshape.21), channel_id=1, replica_groups=mesh['expert'=8,'shard'=32] {'expert'}, dimensions={0} | all-to-all | bytes 524288 | tf_op jit(solution)/shard_map/all_to_all | solution.py:32
  23.7 0.0 all-gather.3.cloned.1.call-update
  23.7 0.0 reduce-scatter.2.cloned.1.call-start
  23.8 76.5 %all-gather.3.cloned.1.call-done = bf16[256,4,4096]{2,1,0:T(4,128)(2,1)} async-done(((bf16[8,4,4096]{2,1,0:T(4,128)(2,1)}), bf16[256,4,4096]{2,1,0:T(4,128)(2,1)}) %all-gather.3.cloned.1.call-update) | async-done | bytes 8388624 | tf_op jit(solution)/shard_map/all_gather | solution.py:33
  100.2 12.5 %reshape.22 = bf16[1024,4096]{1,0:T(8,128)(2,1)} reshape(bf16[256,4,4096]{2,1,0:T(4,128)(2,1)} %all-gather.3.cloned.1.call-done) | data formatting | bytes 16777216 | tf_op jit(solution)/shard_map/reshape | solution.py:35
  112.7 0.0 copy-start.1
  112.7 0.0 copy-start.2
  112.7 8.0 %fusion.3 = f32[1024,384]{1,0:T(8,128)S(1)} fusion(bf16[1024,4096]{1,0:T(8,128)(2,1)} %reshape.22, bf16[1,4096,384]{2,1,0:T(8,128)(2,1)} %param.9), kind=kOutput, calls=%fused_computation.6 | convolution fusion | flops 3221225472 | bytes 13107200 | tf_op jit(solution)/shard_map/dot_general | solution.py:36
  120.7 0.0 copy-done.1
  120.7 0.0 copy-done.2
  120.7 4.6 %multiply_convert_fusion = bf16[1024,384]{1,0:T(8,128)(2,1)S(1)} fusion(f32[1024,384]{1,0:T(8,128)S(1)} %fusion.3, bf16[1024,4096]{1,0:T(8,128)(2,1)S(1)} %copy-done.1, bf16[1,4096,384]{2,1,0:T(8,128)(2,1)S(1)} %copy-done.2), kind=kOutput, calls=%fused_computation.8 | convolution fusion | flops 3223584768 | bytes 13893632 | tf_op jit(solution)/shard_map/dot_general | solution.py:37
  125.3 0.0 copy-done
  125.3 6.7 %convolution_convert_fusion = bf16[1024,4096]{1,0:T(8,128)(2,1)} fusion(bf16[1024,384]{1,0:T(8,128)(2,1)S(1)} %multiply_convert_fusion, bf16[1,384,4096]{2,1,0:T(8,128)(2,1)S(1)} %copy-done), kind=kOutput, calls=%fused_computation | convolution fusion | flops 3225419776 | bytes 12320768 | tf_op jit(solution)/shard_map/dot_general | solution.py:39
  132.0 13.1 %reshape.23 = bf16[32,8,4,4096]{3,2,1,0:T(4,128)(2,1)} reshape(bf16[1024,4096]{1,0:T(8,128)(2,1)} %convolution_convert_fusion) | data formatting | bytes 16777216 | tf_op jit(solution)/shard_map/reshape | solution.py:40
  145.1 15.5 %copy.21 = bf16[32,8,4,4096]{3,1,2,0:T(8,128)(2,1)} copy(bf16[32,8,4,4096]{3,2,1,0:T(4,128)(2,1)} %reshape.23) | data formatting | bytes 16777216 | tf_op jit(solution)/shard_map/optimization_barrier | solution.py:41
  160.5 0.0 reduce-scatter.2.cloned.1.call-update
  160.5 120.9 %reduce-scatter.2.cloned.1.call-done = bf16[1,8,4,4096]{3,1,2,0:T(8,128)(2,1)} async-done(((bf16[32,8,4,4096]{3,1,2,0:T(8,128)(2,1)}), bf16[1,8,4,4096]{3,1,2,0:T(8,128)(2,1)}) %reduce-scatter.2.cloned.1.call-update) | async-done | bytes 262160 | tf_op jit(solution)/shard_map/reduce_scatter | solution.py:42
  281.5 1.2 copy.22
  282.6 11.5 %all_to_all.11 = bf16[1,8,4,4096]{3,2,0,1:T(4,128)(2,1)} all-to-all(bf16[1,8,4,4096]{3,2,0,1:T(4,128)(2,1)S(1)} %copy.22), channel_id=1, replica_groups=mesh['expert'=8,'shard'=32] {'expert'}, dimensions={1} | all-to-all | bytes 524288 | tf_op jit(solution)/shard_map/all_to_all | solution.py:45
  294.1 1.0 reshape.24
  295.1 0.8 fusion.9
  (2 shorter events, 0.0 us)
Async XLA Ops:
  6.5 118.8 %copy-start = (bf16[1,384,4096]{2,1,0:T(8,128)(2,1)S(1)}, bf16[1,384,4096]{2,1,0:T(8,128)(2,1)}, u32[]{:S(2)}) copy-start(bf16[1,384,4096]{2,1,0:T(8,128)(2,1)} %param.11) | copy-start | bytes 9437188
  6.5 93.7 %all-gather.3.cloned.1.call-start = ((), (), s32[]{:S(2)}) async-start(), calls=%async_computation.4 | async-start | bytes 8650752 | tf_op jit(solution)/shard_map/all_gather | solution.py:33
  23.7 257.7 %reduce-scatter.2.cloned.1.call-start = ((), (), s32[]{:S(2)}) async-start(), calls=%async_computation.3 | async-start | bytes 8650752 | tf_op jit(solution)/shard_map/reduce_scatter | solution.py:42
  112.7 8.0 %copy-start.1 = (bf16[1024,4096]{1,0:T(8,128)(2,1)S(1)}, bf16[1024,4096]{1,0:T(8,128)(2,1)}, u32[]{:S(2)}) copy-start(bf16[1024,4096]{1,0:T(8,128)(2,1)} %reshape.22) | copy-start | bytes 25165828
  112.7 8.0 %copy-start.2 = (bf16[1,4096,384]{2,1,0:T(8,128)(2,1)S(1)}, bf16[1,4096,384]{2,1,0:T(8,128)(2,1)}, u32[]{:S(2)}) copy-start(bf16[1,4096,384]{2,1,0:T(8,128)(2,1)} %param.10) | copy-start | bytes 9437188
Sparse Core Ops, SparseCore 0:
  23.8 76.3 all-gather.2
  160.7 120.7 reduce-scatter.1
where the time goes:
time: 304 us; the launch traced here: 303 us
  waiting for transfers between devices  197 us (65%)
  local copies, waits for them, and re-layouts  45.2 us (15%)
  blocking collectives  24.5 us (8%)
  matrix products  21.1 us (7%)
  between operations  13.5 us (4%)
    reduce_scatter x1, waiting for transfers between devices, shards(): lax.psum_scatter(terms.astype(jnp.bfloat16), 'shard', scatter_dimension=0...  121 us
    all_gather x1, waiting for transfers between devices, shards(): row_block = lax.all_gather(arrived[None], 'shard', axis=0, tiled=True)  76.5 us
    optimization_barrier x1, local copies, waits for them, and re-layouts, shards(): terms = lax.optimization_barrier(partials).astype(jnp.float32)  15.5 us
    reshape x1, local copies, waits for them, and re-layouts, shards(): partials = result.astype(jnp.bfloat16).reshape(row_shape)  13.1 us
    all_to_all x1, blocking collectives, shards(): lax.all_to_all(outgoing, 'expert', split_axis=0, concat_axis=0, tiled=True)  13 us
    reshape x1, local copies, waits for them, and re-layouts, shards(): flat_rows = row_block.reshape(-1, row_shape[-1])  12.5 us
    all_to_all x1, blocking collectives, shards(): lax.all_to_all(summed.astype(jnp.bfloat16), 'expert', split_axis=1, conca...  11.5 us
    dot_general x1, matrix products, shards(): jnp.dot(flat_rows, gate_local, preferred_element_type=jnp.float32)  7.97 us
  transfers between devices with their start and end apart: 2, of which 2 were waited for; matrix products, arithmetic and copies ran while one was open for 0% of the time, Pallas kernels for 0%

commit v1 on v0

v1 whole, which is shorter than its diff:
```python
import jax
import jax.numpy as jnp
from jax import lax
from jax.experimental import pallas as pl
from jax.experimental.pallas import tpu as pltpu
from jax.sharding import PartitionSpec as P

MESH = pl.DeviceIdType.MESH
BF = jnp.bfloat16
F32 = jnp.float32
NX, NY, NZ = 4, 4, 8
ORDER = (0, 1, 7, 2, 6, 3, 5, 4)
PLACE = {dz: divmod(p, 2) for p, dz in enumerate(ORDER)}
GROUPS = 4


def kernel(
    tok_ref, ids_ref, rw_ref, wg_ref, wu_ref, wd_ref, out_ref,
    xtok, xinfo, zsend, rows, wg, wu, wd, hid, part, fwd, fin, zsum, ret, mix, xsend, xown, xret,
    x_s, x_r, i_s, i_r, z_s, z_r, a_s, a_r, f_s, f_r, c_s, c_r, b_s, b_r, o_s, o_r, wl, w_s, w_r,
):
    width = tok_ref.shape[1]
    own_hidden = wg_ref.shape[2]
    e = lax.axis_index("expert")
    s = lax.axis_index("shard")
    x, z = e // 2, 2 * (s // 8) + e % 2
    y, c = (s // 2) % NY, s % 2

    def device(dx, dy, dz, dc=0):
        xx, yy, zz = (x + dx) % NX, (y + dy) % NY, (z + dz) % NZ
        return (2 * xx + zz % 2, (zz // 2) * 8 + yy * 2 + (c + dc) % 2)

    def remote(src, dst, send, recv, to):
        copy = pltpu.make_async_remote_copy(
            src_ref=src, dst_ref=dst, send_sem=send, recv_sem=recv, device_id=to, device_id_type=MESH
        )
        copy.start()
        return copy

    sent = []

    cols = pl.ds(0, own_hidden)
    far = pl.ds(own_hidden, own_hidden)
    loads = [
        pltpu.make_async_copy(wg_ref.at[0], wg.at[:, cols], wl.at[0]),
        pltpu.make_async_copy(wu_ref.at[0], wu.at[:, cols], wl.at[1]),
        pltpu.make_async_copy(wd_ref.at[0], wd.at[cols], wl.at[2]),
    ]
    for load in loads:
        load.start()

    barrier = pltpu.get_barrier_semaphore()
    peers = [device(k, 0, 0) for k in range(1, NX)] + [device(0, 0, k) for k in range(1, NZ)]
    peers += [device(0, 1, 0), device(0, 3, 0), device(0, 0, 0, 1)]
    for peer in peers:
        pl.semaphore_signal(barrier, inc=1, device_id=peer, device_id_type=MESH)

    lane = lax.broadcasted_iota(jnp.int32, (2, 128), 1)
    ids = ids_ref[...].astype(F32)
    rw = rw_ref[...]
    ids_wide = jnp.zeros((2, 128), F32)
    rw_wide = jnp.zeros((2, 128), F32)
    for t in range(8):
        ids_wide = jnp.where(lane % 8 == t, ids[:, t : t + 1], ids_wide)
        rw_wide = jnp.where(lane % 8 == t, rw[:, t : t + 1], rw_wide)
    xinfo[0] = jnp.concatenate([ids_wide, rw_wide, jnp.zeros((4, 128), F32)], axis=0)
    xtok[0] = tok_ref[...]

    pl.semaphore_wait(barrier, len(peers))

    info_in, tok_in = [], []
    for k in (1, 3, 2):
        info_in.append(remote(xinfo.at[0], xinfo.at[NX - k], i_s.at[k - 1], i_r.at[k - 1], device(k, 0, 0)))
        tok_in.append(remote(tok_ref, xtok.at[NX - k], x_s.at[k - 1], x_r.at[k - 1], device(k, 0, 0)))
    sent += info_in + tok_in

    partner = device(0, 0, 0, 1)
    weights_in = [
        remote(wg_ref.at[0], wg.at[:, far], w_s.at[0], w_r.at[0], partner),
        remote(wu_ref.at[0], wu.at[:, far], w_s.at[1], w_r.at[1], partner),
        remote(wd_ref.at[0], wd.at[far], w_s.at[2], w_r.at[2], partner),
    ]
    sent += weights_in

    for copy in info_in:
        copy.wait_recv()
    n_rows = 32
    lane = lax.broadcasted_iota(jnp.int32, (1, 128), 1)
    routes = []
    for k in range(4):
        v = jnp.zeros((1, 128), F32)
        for k2 in range(NX):
            v = jnp.where(lane // 8 == k2, xinfo[k2, k : k + 1, :], v)
        routes.append(v)
    id0, id1, w0, w1 = (jnp.broadcast_to(v, (n_rows, 128)) for v in routes)
    row = lax.broadcasted_iota(jnp.int32, (n_rows, 128), 0)
    lane = lax.broadcasted_iota(jnp.int32, (n_rows, 128), 1)
    e_other = e + 1 - 2 * (e % 2)
    wanted = jnp.where(row < 16, jnp.full((n_rows, 128), e), jnp.full((n_rows, 128), e_other)).astype(F32)
    first = id0 == wanted
    member = (first | (id1 == wanted)) & ((row // 4) % 4 == lane // 8)
    a = lax.broadcasted_iota(jnp.int32, (128, 128), 0)
    b = lax.broadcasted_iota(jnp.int32, (128, 128), 1)
    before = jnp.where((a < b) & (a // 8 == b // 8), 1.0, 0.0).astype(BF)
    position = jnp.dot(jnp.where(member, 1.0, 0.0).astype(BF), before, preferred_element_type=F32)
    chosen = member & (position == (row % 4).astype(F32))
    pick = jnp.where(chosen, 1.0, 0.0)
    weighted = jnp.where(chosen, jnp.where(first, w0, w1), 0.0)
    spread = jnp.concatenate([weighted] * 4, axis=0).T
    coarse = spread.astype(BF)
    fine = (spread - coarse.astype(F32)).astype(BF)
    mix[...] = jnp.concatenate([coarse[:32], fine[:32]], axis=0)

    for copy in tok_in:
        copy.wait_recv()
    pick = pick[:, :32].astype(BF)
    step = 1024
    for n in range(0, width, step):
        piece = jnp.dot(pick, xtok[:, :, n : n + step].reshape(32, step), preferred_element_type=F32).astype(BF)
        zsend[0, :, n : n + step] = piece[:16]
        zsend[1, :, n : n + step] = piece[16:]
        rows[0, 0, :, n : n + step] = piece[:16]

    z_in = {}
    for k in (7, 1, 6, 2, 5, 3, 4):
        dz = NZ - k
        g, i = PLACE[dz]
        z_in[dz] = remote(zsend.at[k % 2], rows.at[g, i], z_s.at[dz], z_r.at[dz], device(0, 0, k))
    sent += list(z_in.values())

    up, down = device(0, 1, 0), device(0, 3, 0)
    near_in = {}

    def spread_own(g):
        for i in range(2):
            p = 2 * g + i
            if p:
                z_in[ORDER[p]].wait_recv()
            src = zsend.at[0] if p == 0 else rows.at[g, i]
            near_in[p, 3] = remote(src, rows.at[g, 6 + i], a_s.at[0, p], a_r.at[2, p], up)
            near_in[p, 1] = remote(src, rows.at[g, 2 + i], a_s.at[1, p], a_r.at[0, p], down)
            sent.extend([near_in[p, 3], near_in[p, 1]])

    def spread_on(g):
        p = 2 * g
        near_in[p, 3].wait_recv()
        near_in[p, 2] = remote(rows.at[g, 6], rows.at[g, 4], a_s.at[2, p], a_r.at[1, p], up)
        p += 1
        near_in[p, 1].wait_recv()
        near_in[p, 2] = remote(rows.at[g, 3], rows.at[g, 5], a_s.at[2, p], a_r.at[1, p], down)
        sent.extend([near_in[p - 1, 2], near_in[p, 2]])

    def arrived(g):
        for p, ry in ((2 * g, 1), (2 * g + 1, 3), (2 * g, 2), (2 * g + 1, 2)):
            near_in[p, ry].wait_recv()

    def ffn(g):
        @pl.loop(0, 2 * own_hidden // 256)
        def _(n):
            at = pl.ds(pl.multiple_of(n * 256, 256), 256)
            block = rows[g].reshape(128, width)
            gate = jnp.dot(block, wg[:, at], preferred_element_type=F32)
            upward = jnp.dot(block, wu[:, at], preferred_element_type=F32)
            hid[:, at] = (gate / (1.0 + jnp.exp(-gate)) * upward).astype(BF)

        @pl.loop(0, width // 512)
        def _(n):
            at = pl.ds(pl.multiple_of(n * 512, 512), 512)
            out = jnp.dot(hid[...], wd[:, at], preferred_element_type=F32)
            part[g, :, :, at] = out.astype(BF).reshape(8, 16, 512)

    relay_in, final_in = {}, {}

    def reduce_first(g):
        relay_in[g, 0] = remote(part.at[g, 4], fwd.at[0, g], f_s.at[0, g], f_r.at[0, g], up)
        relay_in[g, 1] = remote(part.at[g, 5], fwd.at[1, g], f_s.at[1, g], f_r.at[1, g], down)
        final_in[g, 0, 1] = remote(part.at[g, 3], fin.at[0, g, 1], c_s.at[0, 2 * g + 1], c_r.at[0, 2 * g + 1], up)
        final_in[g, 1, 0] = remote(part.at[g, 6], fin.at[1, g, 0], c_s.at[1, 2 * g], c_r.at[1, 2 * g], down)

    def reduce_on(g):
        relay_in[g, 0].wait_recv()
        for n in range(0, width, step):
            at = slice(n, n + step)
            part[g, 2, :, at] = (part[g, 2, :, at].astype(F32) + fwd[0, g, :, at].astype(F32)).astype(BF)
        final_in[g, 0, 0] = remote(part.at[g, 2], fin.at[0, g, 0], c_s.at[0, 2 * g], c_r.at[0, 2 * g], up)
        relay_in[g, 1].wait_recv()
        for n in range(0, width, step):
            at = slice(n, n + step)
            part[g, 7, :, at] = (part[g, 7, :, at].astype(F32) + fwd[1, g, :, at].astype(F32)).astype(BF)
        final_in[g, 1, 1] = remote(part.at[g, 7], fin.at[1, g, 1], c_s.at[1, 2 * g + 1], c_r.at[1, 2 * g + 1], down)

    back_in = {}

    def finish(g):
        for i in (1, 0) if g % 2 else (0, 1):
            final_in[g, 0, i].wait_recv()
            final_in[g, 1, i].wait_recv()
            dz = ORDER[2 * g + i]
            for n in range(0, width, step):
                at = slice(n, n + step)
                total = part[g, i, :, at].astype(F32) + fin[0, g, i, :, at].astype(F32) + fin[1, g, i, :, at].astype(F32)
                if dz:
                    zsum[g, i, :, at] = total.astype(BF)
                else:
                    ret[0, :, at] = total.astype(BF)
            if dz:
                slot = NZ - dz
                back_in[slot] = remote(zsum.at[g, i], ret.at[slot], b_s.at[slot], b_r.at[slot], device(0, 0, dz))

    spread_own(0)
    spread_own(1)
    spread_on(0)
    for load in loads:
        load.wait()
    arrived(0)
    for copy in weights_in:
        copy.wait_recv()
    ffn(0)
    reduce_first(0)
    spread_on(1)
    spread_own(2)
    arrived(1)
    ffn(1)
    reduce_first(1)
    spread_on(2)
    spread_own(3)
    spread_on(3)
    arrived(2)
    ffn(2)
    reduce_first(2)
    arrived(3)
    ffn(3)
    reduce_first(3)
    reduce_on(0)
    reduce_on(1)
    finish(0)
    reduce_on(2)
    finish(1)
    reduce_on(3)
    finish(2)
    finish(3)
    sent += list(relay_in.values()) + list(final_in.values()) + list(back_in.values())

    for copy in back_in.values():
        copy.wait_recv()
    for n in range(0, width, step):
        at = slice(n, n + step)
        both = jnp.dot(mix[...], ret[:, :, at].reshape(128, step), preferred_element_type=F32)
        total = both[:32] + both[32:]
        for k in range(1, NX):
            xsend[k - 1, :, at] = total[8 * k : 8 * k + 8].astype(BF)
        xown[:, at] = total[:8]
    x_back = []
    for k in (1, 3, 2):
        x_back.append(remote(xsend.at[k - 1], xret.at[NX - k - 1], o_s.at[k - 1], o_r.at[k - 1], device(k, 0, 0)))
    sent += x_back
    for copy in x_back:
        copy.wait_recv()
    for n in range(0, width, step):
        at = slice(n, n + step)
        total = xown[:, at]
        for k in range(1, NX):
            total = total + xret[k - 1, :, at].astype(F32)
        out_ref[:, at] = total.astype(BF)
    for copy in sent:
        copy.wait_send()


def shards(tokens, expert_ids, route_weights, w_gate, w_up, w_down):
    block, width = tokens.shape
    hidden = w_gate.shape[2]
    dma = pltpu.SemaphoreType.DMA
    vmem = pl.BlockSpec(memory_space=pltpu.VMEM)
    hbm = pl.BlockSpec(memory_space=pl.ANY)
    return pl.pallas_call(
        kernel,
        out_shape=jax.ShapeDtypeStruct((block, width), BF),
        in_specs=[vmem, vmem, vmem, hbm, hbm, hbm],
        out_specs=vmem,
        scratch_shapes=[
            pltpu.VMEM((NX, block, width), BF),
            pltpu.VMEM((NX, 8, 128), F32),
            pltpu.VMEM((2, 16, width), BF),
            pltpu.VMEM((GROUPS, 8, 16, width), BF),
            pltpu.VMEM((width, 2 * hidden), BF),
            pltpu.VMEM((width, 2 * hidden), BF),
            pltpu.VMEM((2 * hidden, width), BF),
            pltpu.VMEM((128, 2 * hidden), BF),
            pltpu.VMEM((GROUPS, 8, 16, width), BF),
            pltpu.VMEM((2, GROUPS, 16, width), BF),
            pltpu.VMEM((2, GROUPS, 2, 16, width), BF),
            pltpu.VMEM((GROUPS, 2, 16, width), BF),
            pltpu.VMEM((NZ, 16, width), BF),
            pltpu.VMEM((64, 128), BF),
            pltpu.VMEM((3, block, width), BF),
            pltpu.VMEM((block, width), F32),
            pltpu.VMEM((3, block, width), BF),
            dma((3,)), dma((3,)), dma((3,)), dma((3,)),
            dma((8,)), dma((8,)),
            dma((3, 8)), dma((3, 8)),
            dma((2, 4)), dma((2, 4)), dma((2, 8)), dma((2, 8)),
            dma((8,)), dma((8,)),
            dma((3,)), dma((3,)),
            dma((3,)), dma((3,)), dma((3,)),
        ],
        compiler_params=pltpu.CompilerParams(
            collective_id=0, has_side_effects=True, vmem_limit_bytes=62 * 1024 * 1024
        ),
    )(tokens, expert_ids.T, route_weights.T, w_gate, w_up, w_down)


def solution(mesh):
    placed = (
        P(("expert", "shard"), None),
        P(("expert", "shard"), None),
        P(("expert", "shard"), None),
        P("expert", None, "shard"),
        P("expert", None, "shard"),
        P("expert", "shard", None),
    )
    return jax.shard_map(
        shards, mesh=mesh, in_specs=placed, out_specs=P(("expert", "shard"), None), check_vma=False
    )
```

time: 304 us -> 117 us (0.38)
  waiting for transfers between devices: 197 us -> 0 us
  Pallas kernels: 0 us -> 114 us
  local copies, waits for them, and re-layouts: 45.2 us -> 1.47 us
  blocking collectives: 24.5 us -> 0 us
  matrix products: 21.1 us -> 0 us
  between operations: 13.5 us -> 0.01 us
    reduce_scatter x1 -> x0, waiting for transfers between devices: 121 us -> none  [shards(): lax.psum_scatter(terms.astype(jnp.bfloat16), 'shard', scatter_dimension=0...]
    pallas_call x0 -> x1, Pallas kernels: none -> 114 us  [shards(): pl.pallas_call(kernel, out_shape=jax.ShapeDtypeStruct((block, width), BF)...]
    all_gather x1 -> x0, waiting for transfers between devices: 76.5 us -> none  [shards(): row_block = lax.all_gather(arrived[None], 'shard', axis=0, tiled=True)]
    reshape x4 -> x0, local copies, waits for them, and re-layouts: 27.4 us -> none  [the longest x1 13.1 us: shards(): partials = result.astype(jnp.bfloat16).reshape(row_shape)]
    all_to_all x2 -> x0, blocking collectives: 24.5 us -> none  [the longest x1 13 us: shards(): lax.all_to_all(outgoing, 'expert', split_axis=0, concat_axis=0, tiled=True)]
    dot_general x5 -> x0, matrix products: 21.1 us -> none  [the longest x1 7.97 us: shards(): jnp.dot(flat_rows, gate_local, preferred_element_type=jnp.float32)]
    optimization_barrier x1 -> x0, local copies, waits for them, and re-layouts: 15.5 us -> none  [shards(): terms = lax.optimization_barrier(partials).astype(jnp.float32)]
  transfers between devices with their start and end apart: 2 -> 0, of which waited for: 2 -> 0; matrix products, arithmetic and copies ran while one was open for 0% -> 0% of each run, Pallas kernels for 0% -> 0%
where the time goes in v1:
time: 117 us; the launch traced here: 115 us
  Pallas kernels  114 us (97%)
  local copies, waits for them, and re-layouts  1.47 us (1%)
    pallas_call x1, Pallas kernels, shards(): pl.pallas_call(kernel, out_shape=jax.ShapeDtypeStruct((block, width), BF)...  114 us

profile of v1, /device:TPU:24, one launch (start us, length us, event | category | flops | bytes accessed | tf_op | source)
XLA Modules:
  0.0 115.0 jit_solution(2504108948121413377)
XLA Ops:
  0.0 113.6 %shard_map.64 = bf16[8,4096]{1,0:T(8,128)(2,1)} custom-call(bf16[8,4096]{1,0:T(8,128)(2,1)} %tok_ref.1, s32[2,8]{1,0:T(2,128)} %bitcast.2, f32[2,8]{1,0:T(2,128)} %bitcast.3, bf16[1,4096,384]{2,1,0:T(8,128)(2,1)} %wg_ref.1, bf16[1,4096,384]{2,1,0:T(8,128)(2,1)} %wu_ref.1, bf16[1,384,4096]{2,1,0:T(8,128)(2,1)} %wd_ref.1), custom_call_target="tpu_custom_call" | custom-call | tf_op jit(solution)/shard_map/pallas_call | solution.py:275
  113.6 1.5 %copy.8 = bf16[8,4096]{1,0:T(8,128)(2,1)} copy(bf16[8,4096]{1,0:T(8,128)(2,1)} %shard_map.64) | data formatting | bytes 131072

commit v2 on v1

--- a/solution.py
+++ b/solution.py
@@ -12,12 +12,13 @@
 ORDER = (0, 1, 7, 2, 6, 3, 5, 4)
 PLACE = {dz: divmod(p, 2) for p, dz in enumerate(ORDER)}
 GROUPS = 4
+PARTS = 4
 
 
 def kernel(
     tok_ref, ids_ref, rw_ref, wg_ref, wu_ref, wd_ref, out_ref,
-    xtok, xinfo, zsend, rows, wg, wu, wd, hid, part, fwd, fin, zsum, ret, mix, xsend, xown, xret,
-    x_s, x_r, i_s, i_r, z_s, z_r, a_s, a_r, f_s, f_r, c_s, c_r, b_s, b_r, o_s, o_r, wl, w_s, w_r,
+    xtok, xinfo, zsend, rows, wg, wu, wd, hid, part, fwd, fin, zsum, ret, mix,
+    x_s, x_r, i_s, i_r, z_s, z_r, a_s, a_r, f_s, f_r, c_s, c_r, b_s, b_r, wl, w_s, w_r,
 ):
     width = tok_ref.shape[1]
     own_hidden = wg_ref.shape[2]
@@ -50,7 +51,7 @@
         load.start()
 
     barrier = pltpu.get_barrier_semaphore()
-    peers = [device(k, 0, 0) for k in range(1, NX)] + [device(0, 0, k) for k in range(1, NZ)]
+    peers = [device(k, 0, 0) for k in range(1, NX)] + [device(0, 0, k) for k in (1, 2, 6, 7)]
     peers += [device(0, 1, 0), device(0, 3, 0), device(0, 0, 0, 1)]
     for peer in peers:
         pl.semaphore_signal(barrier, inc=1, device_id=peer, device_id_type=MESH)
@@ -75,41 +76,41 @@
     sent += info_in + tok_in
 
     partner = device(0, 0, 0, 1)
-    weights_in = [
-        remote(wg_ref.at[0], wg.at[:, far], w_s.at[0], w_r.at[0], partner),
-        remote(wu_ref.at[0], wu.at[:, far], w_s.at[1], w_r.at[1], partner),
-        remote(wd_ref.at[0], wd.at[far], w_s.at[2], w_r.at[2], partner),
-    ]
-    sent += weights_in
+    weights_in = []
+
+    def weight_parts(n):
+        for m in range(len(weights_in), len(weights_in) + n):
+            w, k = m % 3, m // 3
+            src, dst = ((wg_ref, wg), (wu_ref, wu), (wd_ref, wd))[w]
+            size = src.shape[1] // PARTS
+            at = pl.ds(k * size, size)
+            to = dst.at[pl.ds(own_hidden + k * size, size)] if w == 2 else dst.at[at, far]
+            weights_in.append(remote(src.at[0, at], to, w_s.at[w, k], w_r.at[w, k], partner))
+
+    weight_parts(6)
 
     for copy in info_in:
         copy.wait_recv()
     n_rows = 32
     lane = lax.broadcasted_iota(jnp.int32, (1, 128), 1)
     routes = []
-    for k in range(4):
+    for k in range(2):
         v = jnp.zeros((1, 128), F32)
         for k2 in range(NX):
             v = jnp.where(lane // 8 == k2, xinfo[k2, k : k + 1, :], v)
         routes.append(v)
-    id0, id1, w0, w1 = (jnp.broadcast_to(v, (n_rows, 128)) for v in routes)
+    id0, id1 = (jnp.broadcast_to(v, (n_rows, 128)) for v in routes)
     row = lax.broadcasted_iota(jnp.int32, (n_rows, 128), 0)
     lane = lax.broadcasted_iota(jnp.int32, (n_rows, 128), 1)
     e_other = e + 1 - 2 * (e % 2)
     wanted = jnp.where(row < 16, jnp.full((n_rows, 128), e), jnp.full((n_rows, 128), e_other)).astype(F32)
-    first = id0 == wanted
-    member = (first | (id1 == wanted)) & ((row // 4) % 4 == lane // 8)
+    member = ((id0 == wanted) | (id1 == wanted)) & ((row // 4) % 4 == lane // 8)
     a = lax.broadcasted_iota(jnp.int32, (128, 128), 0)
     b = lax.broadcasted_iota(jnp.int32, (128, 128), 1)
     before = jnp.where((a < b) & (a // 8 == b // 8), 1.0, 0.0).astype(BF)
     position = jnp.dot(jnp.where(member, 1.0, 0.0).astype(BF), before, preferred_element_type=F32)
     chosen = member & (position == (row % 4).astype(F32))
     pick = jnp.where(chosen, 1.0, 0.0)
-    weighted = jnp.where(chosen, jnp.where(first, w0, w1), 0.0)
-    spread = jnp.concatenate([weighted] * 4, axis=0).T
-    coarse = spread.astype(BF)
-    fine = (spread - coarse.astype(F32)).astype(BF)
-    mix[...] = jnp.concatenate([coarse[:32], fine[:32]], axis=0)
 
     for copy in tok_in:
         copy.wait_recv()
@@ -122,24 +123,39 @@
         rows[0, 0, :, n : n + step] = piece[:16]
 
     z_in = {}
-    for k in (7, 1, 6, 2, 5, 3, 4):
-        dz = NZ - k
+
+    def send_z(dz, src, sem, at=None):
         g, i = PLACE[dz]
-        z_in[dz] = remote(zsend.at[k % 2], rows.at[g, i], z_s.at[dz], z_r.at[dz], device(0, 0, k))
-    sent += list(z_in.values())
+        dst = rows.at[g, i] if at is None else rows.at[g, i, :, at]
+        hop = (1, -1, 2, -2)[(7, 1, 6, 2).index(dz)] if dz in (7, 1, 6, 2) else (2 if sem in (5, 8) else -2)
+        copy = remote(src, dst, z_s.at[sem], z_r.at[sem], device(0, 0, hop % NZ))
+        z_in.setdefault(dz, []).append(copy)
+        sent.append(copy)
+
+    for dz in (1, 7, 2, 6):
+        send_z(dz, zsend.at[dz % 2], dz)
+
+    def pass_z(dz):
+        g, i = PLACE[dz]
+        if dz in (1, 7):
+            send_z({1: 3, 7: 5}[dz], rows.at[g, i], {1: 3, 7: 5}[dz])
+        if dz in (2, 6):
+            at = pl.ds(0 if dz == 2 else width // 2, width // 2)
+            send_z(4, rows.at[g, i, :, at], {2: 4, 6: 8}[dz], at)
 
     up, down = device(0, 1, 0), device(0, 3, 0)
     near_in = {}
 
-    def spread_own(g):
-        for i in range(2):
-            p = 2 * g + i
-            if p:
-                z_in[ORDER[p]].wait_recv()
-            src = zsend.at[0] if p == 0 else rows.at[g, i]
-            near_in[p, 3] = remote(src, rows.at[g, 6 + i], a_s.at[0, p], a_r.at[2, p], up)
-            near_in[p, 1] = remote(src, rows.at[g, 2 + i], a_s.at[1, p], a_r.at[0, p], down)
-            sent.extend([near_in[p, 3], near_in[p, 1]])
+    def spread_own(p):
+        g, i = divmod(p, 2)
+        dz = ORDER[p]
+        for copy in z_in.get(dz, ()):
+            copy.wait_recv()
+        pass_z(dz)
+        src = zsend.at[0] if p == 0 else rows.at[g, i]
+        near_in[p, 3] = remote(src, rows.at[g, 6 + i], a_s.at[0, p], a_r.at[2, p], up)
+        near_in[p, 1] = remote(src, rows.at[g, 2 + i], a_s.at[1, p], a_r.at[0, p], down)
+        sent.extend([near_in[p, 3], near_in[p, 1]])
 
     def spread_on(g):
         p = 2 * g
@@ -189,79 +205,94 @@
             part[g, 7, :, at] = (part[g, 7, :, at].astype(F32) + fwd[1, g, :, at].astype(F32)).astype(BF)
         final_in[g, 1, 1] = remote(part.at[g, 7], fin.at[1, g, 1], c_s.at[1, 2 * g + 1], c_r.at[1, 2 * g + 1], down)
 
+    row = lax.broadcasted_iota(jnp.int32, (32, 96), 0)
+    col = lax.broadcasted_iota(jnp.int32, (32, 96), 1)
+    fold = jnp.where(((row // 4) % 2 == col // 48) & (row // 8 * 4 + row % 4 == col % 16), 1.0, 0.0).astype(BF)
     back_in = {}
+    half = width // 2
 
     def finish(g):
-        for i in (1, 0) if g % 2 else (0, 1):
+        for i in (1, 0):
             final_in[g, 0, i].wait_recv()
             final_in[g, 1, i].wait_recv()
             dz = ORDER[2 * g + i]
-            for n in range(0, width, step):
-                at = slice(n, n + step)
-                total = part[g, i, :, at].astype(F32) + fin[0, g, i, :, at].astype(F32) + fin[1, g, i, :, at].astype(F32)
-                if dz:
-                    zsum[g, i, :, at] = total.astype(BF)
-                else:
-                    ret[0, :, at] = total.astype(BF)
-            if dz:
-                slot = NZ - dz
-                back_in[slot] = remote(zsum.at[g, i], ret.at[slot], b_s.at[slot], b_r.at[slot], device(0, 0, dz))
+            for n in range(0, half, step):
+                terms = [
+                    ref[:, m + n : m + n + step]
+                    for m in (0, half)
+                    for ref in (part.at[g, i], fin.at[0, g, i], fin.at[1, g, i])
+                ]
+                total = jnp.dot(fold, jnp.concatenate(terms, axis=0), preferred_element_type=F32).astype(BF)
+                for k in range(NX):
+                    if dz or k:
+                        zsum[g, i, k, :, n : n + step] = total[8 * k : 8 * k + 8]
+                    else:
+                        ret[0, 0, :, n : n + step] = total[:8]
+            for k in (2, 1, 3, 0):
+                if dz or k:
+                    at = ((NZ - dz) % NZ, (NX - k) % NX)
+                    back_in[at] = remote(zsum.at[g, i, k], ret.at[at[0], at[1]], b_s.at[at[0], at[1]], b_r.at[at[0], at[1]], device(k, 0, dz))
+
+    row = lax.broadcasted_iota(jnp.int32, (256, 128), 0)
+    lane = lax.broadcasted_iota(jnp.int32, (256, 128), 1)
+    wanted = (2 * ((x + (row // 8) % 4) % NX) + (z + row // 32) % 2).astype(F32)
+    id0, id1, w0, w1 = (jnp.broadcast_to(xinfo[0, k : k + 1, :], (256, 128)) for k in range(4))
+    first = id0 == wanted
+    member = first | (id1 == wanted)
+    position = jnp.dot(jnp.where(member, 1.0, 0.0).astype(BF), before, preferred_element_type=F32)
+    chosen = member & (position == (row % 4).astype(F32)) & (lane // 8 == (row // 4) % 2)
+    spread = jnp.where(chosen, jnp.where(first, w0, w1), 0.0).T
+    coarse = spread.astype(BF)
+    fine = (spread - coarse.astype(F32)).astype(BF)
 
     spread_own(0)
+    weight_parts(3)
+    mix[...] = jnp.concatenate([coarse[:16], fine[:16]], axis=0)
     spread_own(1)
+    spread_own(2)
+    weight_parts(3)
     spread_on(0)
+    spread_own(3)
+    spread_own(4)
     for load in loads:
         load.wait()
     arrived(0)
     for copy in weights_in:
         copy.wait_recv()
     ffn(0)
-    reduce_first(0)
     spread_on(1)
-    spread_own(2)
+    spread_own(5)
+    spread_own(6)
     arrived(1)
     ffn(1)
-    reduce_first(1)
     spread_on(2)
-    spread_own(3)
-    spread_on(3)
+    spread_own(7)
     arrived(2)
     ffn(2)
+    spread_on(3)
     reduce_first(2)
     arrived(3)
     ffn(3)
+    reduce_on(2)
     reduce_first(3)
+    reduce_on(3)
+    reduce_first(1)
+    reduce_first(0)
+    finish(2)
+    reduce_on(1)
+    finish(3)
     reduce_on(0)
-    reduce_on(1)
+    finish(1)
     finish(0)
-    reduce_on(2)
-    finish(1)
-    reduce_on(3)
-    finish(2)
-    finish(3)
-    sent += list(relay_in.values()) + list(final_in.values()) + list(back_in.values())
+    sent += weights_in + list(relay_in.values()) + list(final_in.values()) + list(back_in.values())
 
     for copy in back_in.values():
         copy.wait_recv()
-    for n in range(0, width, step):
-        at = slice(n, n + step)
-        both = jnp.dot(mix[...], ret[:, :, at].reshape(128, step), preferred_element_type=F32)
-        total = both[:32] + both[32:]
-        for k in range(1, NX):
-            xsend[k - 1, :, at] = total[8 * k : 8 * k + 8].astype(BF)
-        xown[:, at] = total[:8]
-    x_back = []
-    for k in (1, 3, 2):
-        x_back.append(remote(xsend.at[k - 1], xret.at[NX - k - 1], o_s.at[k - 1], o_r.at[k - 1], device(k, 0, 0)))
-    sent += x_back
-    for copy in x_back:
-        copy.wait_recv()
-    for n in range(0, width, step):
-        at = slice(n, n + step)
-        total = xown[:, at]
-        for k in range(1, NX):
-            total = total + xret[k - 1, :, at].astype(F32)
-        out_ref[:, at] = total.astype(BF)
+    for n in range(0, half, step):
+        both = jnp.dot(mix[...], ret[:, :, :, n : n + step].reshape(256, step), preferred_element_type=F32)
+        total = (both[:16] + both[16:]).astype(BF)
+        out_ref[:, n : n + step] = total[:8]
+        out_ref[:, half + n : half + n + step] = total[8:]
     for copy in sent:
         copy.wait_send()
 
@@ -289,19 +320,15 @@
             pltpu.VMEM((GROUPS, 8, 16, width), BF),
             pltpu.VMEM((2, GROUPS, 16, width), BF),
             pltpu.VMEM((2, GROUPS, 2, 16, width), BF),
-            pltpu.VMEM((GROUPS, 2, 16, width), BF),
-            pltpu.VMEM((NZ, 16, width), BF),
-            pltpu.VMEM((64, 128), BF),
-            pltpu.VMEM((3, block, width), BF),
-            pltpu.VMEM((block, width), F32),
-            pltpu.VMEM((3, block, width), BF),
+            pltpu.VMEM((GROUPS, 2, NX, 8, width // 2), BF),
+            pltpu.VMEM((NZ, NX, 8, width // 2), BF),
+            pltpu.VMEM((32, 256), BF),
             dma((3,)), dma((3,)), dma((3,)), dma((3,)),
-            dma((8,)), dma((8,)),
+            dma((9,)), dma((9,)),
             dma((3, 8)), dma((3, 8)),
             dma((2, 4)), dma((2, 4)), dma((2, 8)), dma((2, 8)),
-            dma((8,)), dma((8,)),
-            dma((3,)), dma((3,)),
-            dma((3,)), dma((3,)), dma((3,)),
+            dma((NZ, NX)), dma((NZ, NX)),
+            dma((3,)), dma((3, PARTS)), dma((3, PARTS)),
         ],
         compiler_params=pltpu.CompilerParams(
             collective_id=0, has_side_effects=True, vmem_limit_bytes=62 * 1024 * 1024

time: 117 us -> 100 us (0.85); the launches traced: 115 us -> 100 us
  Pallas kernels: 114 us -> 98.8 us
    pallas_call x1, Pallas kernels: 114 us -> 98.8 us  [shards(): pl.pallas_call(kernel, out_shape=jax.ShapeDtypeStruct((block, width), BF)...]
where the time goes in v2:
time: 100 us
  Pallas kernels  98.8 us (99%)
  local copies, waits for them, and re-layouts  1.47 us (1%)
    pallas_call x1, Pallas kernels, shards(): pl.pallas_call(kernel, out_shape=jax.ShapeDtypeStruct((block, width), BF)...  98.8 us

profile of v2, /device:TPU:24, one launch (start us, length us, event | category | flops | bytes accessed | tf_op | source)
XLA Modules:
  0.0 100.3 jit_solution(4769542477386186737)
XLA Ops:
  0.0 98.8 %shard_map.64 = bf16[8,4096]{1,0:T(8,128)(2,1)} custom-call(bf16[8,4096]{1,0:T(8,128)(2,1)} %tok_ref.1, s32[2,8]{1,0:T(2,128)} %bitcast.2, f32[2,8]{1,0:T(2,128)} %bitcast.3, bf16[1,4096,384]{2,1,0:T(8,128)(2,1)} %wg_ref.1, bf16[1,4096,384]{2,1,0:T(8,128)(2,1)} %wu_ref.1, bf16[1,384,4096]{2,1,0:T(8,128)(2,1)} %wd_ref.1), custom_call_target="tpu_custom_call" | custom-call | tf_op jit(solution)/shard_map/pallas_call | solution.py:306
  98.8 1.5 %copy.8 = bf16[8,4096]{1,0:T(8,128)(2,1)} copy(bf16[8,4096]{1,0:T(8,128)(2,1)} %shard_map.64) | data formatting | bytes 131072

commit v3 on v2

--- a/solution.py
+++ b/solution.py
@@ -9,16 +9,18 @@
 BF = jnp.bfloat16
 F32 = jnp.float32
 NX, NY, NZ = 4, 4, 8
-ORDER = (0, 1, 7, 2, 6, 3, 5, 4)
+ORDER = (0, 1, 7, 2, 5, 4, 6, 3)
 PLACE = {dz: divmod(p, 2) for p, dz in enumerate(ORDER)}
 GROUPS = 4
+STRAIGHT = (0, 7, 1, 6)
+SUMMED = (3, 4, 2, 5)
 PARTS = 4
 
 
 def kernel(
     tok_ref, ids_ref, rw_ref, wg_ref, wu_ref, wd_ref, out_ref,
-    xtok, xinfo, zsend, rows, wg, wu, wd, hid, part, fwd, fin, zsum, ret, mix,
-    x_s, x_r, i_s, i_r, z_s, z_r, a_s, a_r, f_s, f_r, c_s, c_r, b_s, b_r, wl, w_s, w_r,
+    xtok, xinfo, zsend, rows, wg, wu, wd, hid, part, fwd, fin, zsum, ret, mix, yinfo, zback, near, ymix, ysum, yown, yret,
+    x_s, x_r, i_s, i_r, z_s, z_r, a_s, a_r, f_s, f_r, c_s, c_r, b_s, b_r, n_s, n_r, j_s, j_r, y_s, y_r, wl, w_s, w_r,
 ):
     width = tok_ref.shape[1]
     own_hidden = wg_ref.shape[2]
@@ -52,7 +54,7 @@
 
     barrier = pltpu.get_barrier_semaphore()
     peers = [device(k, 0, 0) for k in range(1, NX)] + [device(0, 0, k) for k in (1, 2, 6, 7)]
-    peers += [device(0, 1, 0), device(0, 3, 0), device(0, 0, 0, 1)]
+    peers += [device(0, k, 0) for k in range(1, NY)] + [device(0, 0, 0, 1)]
     for peer in peers:
         pl.semaphore_signal(barrier, inc=1, device_id=peer, device_id_type=MESH)
 
@@ -73,7 +75,10 @@
     for k in (1, 3, 2):
         info_in.append(remote(xinfo.at[0], xinfo.at[NX - k], i_s.at[k - 1], i_r.at[k - 1], device(k, 0, 0)))
         tok_in.append(remote(tok_ref, xtok.at[NX - k], x_s.at[k - 1], x_r.at[k - 1], device(k, 0, 0)))
-    sent += info_in + tok_in
+    yinfo_in = [
+        remote(xinfo.at[0], yinfo.at[NY - k], j_s.at[k - 1], j_r.at[k - 1], device(0, k, 0)) for k in (1, 3, 2)
+    ]
+    sent += info_in + tok_in + yinfo_in
 
     partner = device(0, 0, 0, 1)
     weights_in = []
@@ -157,20 +162,18 @@
         near_in[p, 1] = remote(src, rows.at[g, 2 + i], a_s.at[1, p], a_r.at[0, p], down)
         sent.extend([near_in[p, 3], near_in[p, 1]])
 
-    def spread_on(g):
-        p = 2 * g
-        near_in[p, 3].wait_recv()
-        near_in[p, 2] = remote(rows.at[g, 6], rows.at[g, 4], a_s.at[2, p], a_r.at[1, p], up)
-        p += 1
-        near_in[p, 1].wait_recv()
-        near_in[p, 2] = remote(rows.at[g, 3], rows.at[g, 5], a_s.at[2, p], a_r.at[1, p], down)
-        sent.extend([near_in[p - 1, 2], near_in[p, 2]])
+    def spread_on(p):
+        g, i = divmod(p, 2)
+        came, to, ry = (3, up, 6) if i == 0 else (1, down, 3)
+        near_in[p, came].wait_recv()
+        near_in[p, 2] = remote(rows.at[g, ry], rows.at[g, 4 + i], a_s.at[2, p], a_r.at[1, p], to)
+        sent.append(near_in[p, 2])
 
     def arrived(g):
         for p, ry in ((2 * g, 1), (2 * g + 1, 3), (2 * g, 2), (2 * g + 1, 2)):
             near_in[p, ry].wait_recv()
 
-    def ffn(g):
+    def ffn_up(g):
         @pl.loop(0, 2 * own_hidden // 256)
         def _(n):
             at = pl.ds(pl.multiple_of(n * 256, 256), 256)
@@ -179,6 +182,7 @@
             upward = jnp.dot(block, wu[:, at], preferred_element_type=F32)
             hid[:, at] = (gate / (1.0 + jnp.exp(-gate)) * upward).astype(BF)
 
+    def ffn_down(g):
         @pl.loop(0, width // 512)
         def _(n):
             at = pl.ds(pl.multiple_of(n * 512, 512), 512)
@@ -188,22 +192,22 @@
     relay_in, final_in = {}, {}
 
     def reduce_first(g):
-        relay_in[g, 0] = remote(part.at[g, 4], fwd.at[0, g], f_s.at[0, g], f_r.at[0, g], up)
-        relay_in[g, 1] = remote(part.at[g, 5], fwd.at[1, g], f_s.at[1, g], f_r.at[1, g], down)
-        final_in[g, 0, 1] = remote(part.at[g, 3], fin.at[0, g, 1], c_s.at[0, 2 * g + 1], c_r.at[0, 2 * g + 1], up)
-        final_in[g, 1, 0] = remote(part.at[g, 6], fin.at[1, g, 0], c_s.at[1, 2 * g], c_r.at[1, 2 * g], down)
+        relay_in[g, 0] = remote(part.at[g, 4], fwd.at[0, g - 2], f_s.at[0, g - 2], f_r.at[0, g - 2], up)
+        relay_in[g, 1] = remote(part.at[g, 5], fwd.at[1, g - 2], f_s.at[1, g - 2], f_r.at[1, g - 2], down)
+        final_in[g, 0, 1] = remote(part.at[g, 3], fin.at[0, g - 2, 1], c_s.at[0, 2 * g - 3], c_r.at[0, 2 * g - 3], up)
+        final_in[g, 1, 0] = remote(part.at[g, 6], fin.at[1, g - 2, 0], c_s.at[1, 2 * g - 4], c_r.at[1, 2 * g - 4], down)
 
     def reduce_on(g):
         relay_in[g, 0].wait_recv()
         for n in range(0, width, step):
             at = slice(n, n + step)
-            part[g, 2, :, at] = (part[g, 2, :, at].astype(F32) + fwd[0, g, :, at].astype(F32)).astype(BF)
-        final_in[g, 0, 0] = remote(part.at[g, 2], fin.at[0, g, 0], c_s.at[0, 2 * g], c_r.at[0, 2 * g], up)
+            part[g, 2, :, at] = (part[g, 2, :, at].astype(F32) + fwd[0, g - 2, :, at].astype(F32)).astype(BF)
+        final_in[g, 0, 0] = remote(part.at[g, 2], fin.at[0, g - 2, 0], c_s.at[0, 2 * g - 4], c_r.at[0, 2 * g - 4], up)
         relay_in[g, 1].wait_recv()
         for n in range(0, width, step):
             at = slice(n, n + step)
-            part[g, 7, :, at] = (part[g, 7, :, at].astype(F32) + fwd[1, g, :, at].astype(F32)).astype(BF)
-        final_in[g, 1, 1] = remote(part.at[g, 7], fin.at[1, g, 1], c_s.at[1, 2 * g + 1], c_r.at[1, 2 * g + 1], down)
+            part[g, 7, :, at] = (part[g, 7, :, at].astype(F32) + fwd[1, g - 2, :, at].astype(F32)).astype(BF)
+        final_in[g, 1, 1] = remote(part.at[g, 7], fin.at[1, g - 2, 1], c_s.at[1, 2 * g - 3], c_r.at[1, 2 * g - 3], down)
 
     row = lax.broadcasted_iota(jnp.int32, (32, 96), 0)
     col = lax.broadcasted_iota(jnp.int32, (32, 96), 1)
@@ -216,83 +220,140 @@
             final_in[g, 0, i].wait_recv()
             final_in[g, 1, i].wait_recv()
             dz = ORDER[2 * g + i]
+            slot = SUMMED.index(NZ - dz)
             for n in range(0, half, step):
                 terms = [
                     ref[:, m + n : m + n + step]
                     for m in (0, half)
-                    for ref in (part.at[g, i], fin.at[0, g, i], fin.at[1, g, i])
+                    for ref in (part.at[g, i], fin.at[0, g - 2, i], fin.at[1, g - 2, i])
                 ]
                 total = jnp.dot(fold, jnp.concatenate(terms, axis=0), preferred_element_type=F32).astype(BF)
                 for k in range(NX):
-                    if dz or k:
-                        zsum[g, i, k, :, n : n + step] = total[8 * k : 8 * k + 8]
+                    zsum[g - 2, i, k, :, n : n + step] = total[8 * k : 8 * k + 8]
+            for k in (2, 1, 3, 0):
+                to = (NX - k) % NX
+                back_in[slot, to] = remote(zsum.at[g - 2, i, k], ret.at[slot, to], b_s.at[slot, to], b_r.at[slot, to], device(k, 0, dz))
+
+    row = lax.broadcasted_iota(jnp.int32, (32, 32), 0)
+    col = lax.broadcasted_iota(jnp.int32, (32, 32), 1)
+    fold_one = jnp.where(((row // 4) % 2 == col // 16) & (row // 8 * 4 + row % 4 == col % 16), 1.0, 0.0).astype(BF)
+    straight_in = {}
+
+    def go_back(g):
+        for i in range(2):
+            dz = ORDER[2 * g + i]
+            slot = STRAIGHT.index((NZ - dz) % NZ)
+            for ry in range(NY):
+                for n in range(0, half, step):
+                    terms = [part[g, 2 * ry + i, :, m + n : m + n + step] for m in (0, half)]
+                    moved = jnp.dot(fold_one, jnp.concatenate(terms, axis=0), preferred_element_type=F32).astype(BF)
+                    for k in range(NX):
+                        if dz or k:
+                            zback[g, i, k, ry, :, n : n + step] = moved[8 * k : 8 * k + 8]
+                        else:
+                            near[0, 0, ry, :, n : n + step] = moved[:8]
+            for k in (2, 1, 3, 0):
+                to = (NX - k) % NX
+                if dz or k:
+                    straight_in[slot, to] = remote(zback.at[g, i, k], near.at[slot, to], n_s.at[slot, to], n_r.at[slot, to], device(k, 0, dz))
+
+    def token_mix(info, flip):
+        row = lax.broadcasted_iota(jnp.int32, (128, 128), 0)
+        lane = lax.broadcasted_iota(jnp.int32, (128, 128), 1)
+        wanted = (2 * ((x + (row // 8) % 4) % NX) + (z + (row // 32 + 1) // 2 + flip) % 2).astype(F32)
+        id0, id1, w0, w1 = (jnp.broadcast_to(info[k : k + 1, :], (128, 128)) for k in range(4))
+        first = id0 == wanted
+        member = first | (id1 == wanted)
+        position = jnp.dot(jnp.where(member, 1.0, 0.0).astype(BF), before, preferred_element_type=F32)
+        chosen = member & (position == (row % 4).astype(F32)) & (lane // 8 == (row // 4) % 2)
+        spread = jnp.where(chosen, jnp.where(first, w0, w1), 0.0).T
+        coarse = spread.astype(BF)
+        fine = (spread - coarse.astype(F32)).astype(BF)
+        return jnp.concatenate([coarse[:16], fine[:16]], axis=0)
+
+    y_back = []
+
+    def sum_straight():
+        for copy in straight_in.values():
+            copy.wait_recv()
+        for ry in (2, 1, 3, 0):
+            for n in range(0, half, step):
+                both = jnp.dot(ymix[ry], near[:, :, ry, :, n : n + step].reshape(128, step), preferred_element_type=F32)
+                total = both[:16] + both[16:]
+                for m in range(2):
+                    at = slice(m * half + n, m * half + n + step)
+                    if ry:
+                        ysum[ry - 1, :, at] = total[8 * m : 8 * m + 8].astype(BF)
                     else:
-                        ret[0, 0, :, n : n + step] = total[:8]
-            for k in (2, 1, 3, 0):
-                if dz or k:
-                    at = ((NZ - dz) % NZ, (NX - k) % NX)
-                    back_in[at] = remote(zsum.at[g, i, k], ret.at[at[0], at[1]], b_s.at[at[0], at[1]], b_r.at[at[0], at[1]], device(k, 0, dz))
-
-    row = lax.broadcasted_iota(jnp.int32, (256, 128), 0)
-    lane = lax.broadcasted_iota(jnp.int32, (256, 128), 1)
-    wanted = (2 * ((x + (row // 8) % 4) % NX) + (z + row // 32) % 2).astype(F32)
-    id0, id1, w0, w1 = (jnp.broadcast_to(xinfo[0, k : k + 1, :], (256, 128)) for k in range(4))
-    first = id0 == wanted
-    member = first | (id1 == wanted)
-    position = jnp.dot(jnp.where(member, 1.0, 0.0).astype(BF), before, preferred_element_type=F32)
-    chosen = member & (position == (row % 4).astype(F32)) & (lane // 8 == (row // 4) % 2)
-    spread = jnp.where(chosen, jnp.where(first, w0, w1), 0.0).T
-    coarse = spread.astype(BF)
-    fine = (spread - coarse.astype(F32)).astype(BF)
+                        yown[:, at] = total[8 * m : 8 * m + 8]
+            if ry:
+                y_back.append(remote(ysum.at[ry - 1], yret.at[NY - ry - 1], y_s.at[ry - 1], y_r.at[ry - 1], device(0, ry, 0)))
 
     spread_own(0)
     weight_parts(3)
-    mix[...] = jnp.concatenate([coarse[:16], fine[:16]], axis=0)
+    mix[...] = token_mix(xinfo[0], 1)
     spread_own(1)
     spread_own(2)
     weight_parts(3)
     spread_on(0)
+    spread_on(1)
     spread_own(3)
-    spread_own(4)
+    spread_own(6)
     for load in loads:
         load.wait()
     arrived(0)
     for copy in weights_in:
         copy.wait_recv()
-    ffn(0)
-    spread_on(1)
+    ffn_up(0)
+    spread_on(2)
+    spread_own(4)
+    ffn_down(0)
+    spread_on(3)
+    go_back(0)
     spread_own(5)
-    spread_own(6)
+    spread_own(7)
     arrived(1)
-    ffn(1)
-    spread_on(2)
-    spread_own(7)
+    ffn_up(1)
+    spread_on(4)
+    spread_on(6)
+    spread_on(5)
+    ffn_down(1)
+    go_back(1)
+    spread_on(7)
+    for copy in yinfo_in:
+        copy.wait_recv()
+    ymix[0] = token_mix(xinfo[0], 0)
+    for k in range(1, NY):
+        ymix[k] = token_mix(yinfo[k], 0)
     arrived(2)
-    ffn(2)
-    spread_on(3)
+    ffn_up(2)
+    ffn_down(2)
     reduce_first(2)
     arrived(3)
-    ffn(3)
+    ffn_up(3)
+    ffn_down(3)
     reduce_on(2)
     reduce_first(3)
+    finish(2)
     reduce_on(3)
-    reduce_first(1)
-    reduce_first(0)
-    finish(2)
-    reduce_on(1)
     finish(3)
-    reduce_on(0)
-    finish(1)
-    finish(0)
+    sum_straight()
     sent += weights_in + list(relay_in.values()) + list(final_in.values()) + list(back_in.values())
-
+    sent += list(straight_in.values()) + y_back
+
+    for copy in y_back:
+        copy.wait_recv()
     for copy in back_in.values():
         copy.wait_recv()
     for n in range(0, half, step):
-        both = jnp.dot(mix[...], ret[:, :, :, n : n + step].reshape(256, step), preferred_element_type=F32)
-        total = (both[:16] + both[16:]).astype(BF)
-        out_ref[:, n : n + step] = total[:8]
-        out_ref[:, half + n : half + n + step] = total[8:]
+        both = jnp.dot(mix[...], ret[:, :, :, n : n + step].reshape(128, step), preferred_element_type=F32)
+        total = both[:16] + both[16:]
+        for m in range(2):
+            at = slice(m * half + n, m * half + n + step)
+            rest = yown[:, at]
+            for k in range(NY - 1):
+                rest = rest + yret[k, :, at].astype(F32)
+            out_ref[:, at] = (total[8 * m : 8 * m + 8] + rest).astype(BF)
     for copy in sent:
         copy.wait_send()
 
@@ -318,16 +379,25 @@
             pltpu.VMEM((2 * hidden, width), BF),
             pltpu.VMEM((128, 2 * hidden), BF),
             pltpu.VMEM((GROUPS, 8, 16, width), BF),
-            pltpu.VMEM((2, GROUPS, 16, width), BF),
-            pltpu.VMEM((2, GROUPS, 2, 16, width), BF),
-            pltpu.VMEM((GROUPS, 2, NX, 8, width // 2), BF),
-            pltpu.VMEM((NZ, NX, 8, width // 2), BF),
-            pltpu.VMEM((32, 256), BF),
+            pltpu.VMEM((2, 2, 16, width), BF),
+            pltpu.VMEM((2, 2, 2, 16, width), BF),
+            pltpu.VMEM((2, 2, NX, 8, width // 2), BF),
+            pltpu.VMEM((4, NX, 8, width // 2), BF),
+            pltpu.VMEM((32, 128), BF),
+            pltpu.VMEM((NY, 8, 128), F32),
+            pltpu.VMEM((2, 2, NX, NY, 8, width // 2), BF),
+            pltpu.VMEM((4, NX, NY, 8, width // 2), BF),
+            pltpu.VMEM((NY, 32, 128), BF),
+            pltpu.VMEM((3, block, width), BF),
+            pltpu.VMEM((block, width), F32),
+            pltpu.VMEM((3, block, width), BF),
             dma((3,)), dma((3,)), dma((3,)), dma((3,)),
             dma((9,)), dma((9,)),
             dma((3, 8)), dma((3, 8)),
-            dma((2, 4)), dma((2, 4)), dma((2, 8)), dma((2, 8)),
-            dma((NZ, NX)), dma((NZ, NX)),
+            dma((2, 2)), dma((2, 2)), dma((2, 4)), dma((2, 4)),
+            dma((4, NX)), dma((4, NX)),
+            dma((4, NX)), dma((4, NX)),
+            dma((3,)), dma((3,)), dma((3,)), dma((3,)),
             dma((3,)), dma((3, PARTS)), dma((3, PARTS)),
         ],
         compiler_params=pltpu.CompilerParams(

time: 100 us -> 88.1 us (0.88)
  Pallas kernels: 98.8 us -> 86.4 us
    pallas_call x1, Pallas kernels: 98.8 us -> 86.4 us  [shards(): pl.pallas_call(kernel, out_shape=jax.ShapeDtypeStruct((block, width), BF)...]
where the time goes in v3:
time: 88.1 us; the launch traced here: 87.9 us
  Pallas kernels  86.4 us (98%)
  local copies, waits for them, and re-layouts  1.47 us (2%)
    pallas_call x1, Pallas kernels, shards(): pl.pallas_call(kernel, out_shape=jax.ShapeDtypeStruct((block, width), BF)...  86.4 us

profile of v3, /device:TPU:24, one launch (start us, length us, event | category | flops | bytes accessed | tf_op | source)
XLA Modules:
  0.0 87.9 jit_solution(1359502023566504330)
XLA Ops:
  0.0 86.4 %shard_map.64 = bf16[8,4096]{1,0:T(8,128)(2,1)} custom-call(bf16[8,4096]{1,0:T(8,128)(2,1)} %tok_ref.1, s32[2,8]{1,0:T(2,128)} %bitcast.2, f32[2,8]{1,0:T(2,128)} %bitcast.3, bf16[1,4096,384]{2,1,0:T(8,128)(2,1)} %wg_ref.1, bf16[1,4096,384]{2,1,0:T(8,128)(2,1)} %wu_ref.1, bf16[1,384,4096]{2,1,0:T(8,128)(2,1)} %wd_ref.1), custom_call_target="tpu_custom_call" | custom-call | tf_op jit(solution)/shard_map/pallas_call | solution.py:367
  86.4 1.5 %copy.8 = bf16[8,4096]{1,0:T(8,128)(2,1)} copy(bf16[8,4096]{1,0:T(8,128)(2,1)} %shard_map.64) | data formatting | bytes 131072

commit v4 on v3

v4 whole, which is shorter than its diff:
```python
import jax
import jax.numpy as jnp
from jax import lax
from jax.experimental import pallas as pl
from jax.experimental.pallas import tpu as pltpu
from jax.sharding import PartitionSpec as P

MESH = pl.DeviceIdType.MESH
BF = jnp.bfloat16
F32 = jnp.float32
NX, NY, NZ = 4, 4, 8
ORDER = (0, 1, 7, 2, 5, 4, 6, 3)
PLACE = {dz: divmod(p, 2) for p, dz in enumerate(ORDER)}
GROUPS = 4
STRAIGHT = (0, 7, 1, 6)
SUMMED = (3, 4, 2, 5)
PARTS = 4
POOL = 40
DOWN = 2048


def kernel(
    tok_ref, ids_ref, rw_ref, wg_ref, wu_ref, wd_ref, out_ref,
    xtok, xinfo, zsend, rows, wg, wu, wd, hid, part, fwd, fin, zsum, ret, mix, yinfo, zback, near, ymix, ysum, yown, yret, ids_in, rw_in,
    send, all_s, x_r, i_r, z_r, a_r, d_r, f_r, c_r, b_r, n_r, j_r, y_r, t_s, wl, w_r,
):
    width = tok_ref.shape[1]
    own = [
        pltpu.make_async_copy(ids_ref, ids_in, t_s.at[0]),
        pltpu.make_async_copy(rw_ref, rw_in, t_s.at[1]),
        pltpu.make_async_copy(tok_ref, xtok.at[0], t_s.at[2]),
    ]
    for copy in own:
        copy.start()
    own_hidden = wg_ref.shape[2]
    e = lax.axis_index("expert")
    s = lax.axis_index("shard")
    x, z = e // 2, 2 * (s // 8) + e % 2
    y, c = (s // 2) % NY, s % 2

    def device(dx, dy, dz, dc=0):
        xx, yy, zz = (x + dx) % NX, (y + dy) % NY, (z + dz) % NZ
        return (2 * xx + zz % 2, (zz // 2) * 8 + yy * 2 + (c + dc) % 2)

    sent = []

    def remote(src, dst, recv, to, own_send=None):
        n = len(sent)
        if own_send is None and n >= POOL:
            sent[n - POOL].wait_send()
        copy = pltpu.make_async_remote_copy(
            src_ref=src, dst_ref=dst, send_sem=send.at[n % POOL] if own_send is None else own_send, recv_sem=recv, device_id=to, device_id_type=MESH
        )
        copy.start()
        if own_send is None:
            sent.append(copy)
        return copy

    def landed(ref, sem):
        pltpu.make_async_copy(ref, ref, sem).wait()

    cols = pl.ds(0, own_hidden)
    far = pl.ds(own_hidden, own_hidden)
    loads = [
        pltpu.make_async_copy(wg_ref.at[0], wg.at[:, cols], wl.at[0]),
        pltpu.make_async_copy(wu_ref.at[0], wu.at[:, cols], wl.at[1]),
        pltpu.make_async_copy(wd_ref.at[0], wd.at[cols], wl.at[2]),
    ]

    barrier = pltpu.get_barrier_semaphore()
    peers = [device(k, 0, 0) for k in range(1, NX)] + [device(0, 0, k) for k in (1, 2, 6, 7)]
    peers += [device(0, k, 0) for k in range(1, NY)] + [device(0, 0, 0, 1)]
    for peer in peers:
        pl.semaphore_signal(barrier, inc=1, device_id=peer, device_id_type=MESH)

    for load in loads:
        load.start()
    for copy in own:
        copy.wait()

    lane = lax.broadcasted_iota(jnp.int32, (2, 128), 1)
    ids = ids_in[...].astype(F32)
    rw = rw_in[...]
    ids_wide = jnp.zeros((2, 128), F32)
    rw_wide = jnp.zeros((2, 128), F32)
    for t in range(8):
        ids_wide = jnp.where(lane % 8 == t, ids[:, t : t + 1], ids_wide)
        rw_wide = jnp.where(lane % 8 == t, rw[:, t : t + 1], rw_wide)
    xinfo[0] = jnp.concatenate([ids_wide, rw_wide, jnp.zeros((4, 128), F32)], axis=0)

    pl.semaphore_wait(barrier, len(peers))

    for k in (1, 3, 2):
        remote(xinfo.at[0], xinfo.at[NX - k], i_r.at[0], device(k, 0, 0))
    half = width // 2
    halves = (pl.ds(0, half), pl.ds(half, half))
    for h, at in enumerate(halves):
        for k in (1, 3, 2):
            remote(xtok.at[0, :, at], xtok.at[NX - k, :, at], x_r.at[h], device(k, 0, 0))
    for k in (1, 3, 2):
        remote(xinfo.at[0], yinfo.at[NY - k], j_r.at[0], device(0, k, 0))

    partner = device(0, 0, 0, 1)
    weights_in = []

    def weight_parts(n):
        for m in range(len(weights_in), len(weights_in) + n):
            w, k = m % 3, m // 3
            src, dst = ((wg_ref, wg), (wu_ref, wu), (wd_ref, wd))[w]
            size = src.shape[1] // PARTS
            at = pl.ds(k * size, size)
            to = dst.at[pl.ds(own_hidden + k * size, size)] if w == 2 else dst.at[at, far]
            weights_in.append(remote(src.at[0, at], to, w_r.at[w], partner))

    weight_parts(6)

    landed(xinfo.at[pl.ds(1, 3)], i_r.at[0])
    n_rows = 32
    lane = lax.broadcasted_iota(jnp.int32, (1, 128), 1)
    routes = []
    for k in range(2):
        v = jnp.zeros((1, 128), F32)
        for k2 in range(NX):
            v = jnp.where(lane // 8 == k2, xinfo[k2, k : k + 1, :], v)
        routes.append(v)
    id0, id1 = (jnp.broadcast_to(v, (n_rows, 128)) for v in routes)
    row = lax.broadcasted_iota(jnp.int32, (n_rows, 128), 0)
    lane = lax.broadcasted_iota(jnp.int32, (n_rows, 128), 1)
    e_other = e + 1 - 2 * (e % 2)
    wanted = jnp.where(row < 16, jnp.full((n_rows, 128), e), jnp.full((n_rows, 128), e_other)).astype(F32)
    member = ((id0 == wanted) | (id1 == wanted)) & ((row // 4) % 4 == lane // 8)
    a = lax.broadcasted_iota(jnp.int32, (128, 128), 0)
    b = lax.broadcasted_iota(jnp.int32, (128, 128), 1)
    before = jnp.where((a < b) & (a // 8 == b // 8), 1.0, 0.0).astype(BF)
    position = jnp.dot(jnp.where(member, 1.0, 0.0).astype(BF), before, preferred_element_type=F32)
    chosen = member & (position == (row % 4).astype(F32))
    pick = jnp.where(chosen, 1.0, 0.0)

    up, down = device(0, 1, 0), device(0, 3, 0)
    z_in, near_in = {}, {}

    def send_z(dz, src, sem, hop, at=None):
        g, i = PLACE[dz]
        dst = rows.at[g, i] if at is None else rows.at[g, i, :, at]
        z_in.setdefault(dz, []).append(remote(src, dst, z_r.at[sem], device(0, 0, hop % NZ)))

    def send_y(p, h=None):
        g, i = divmod(p, 2)
        src = rows.at[g, i] if p else zsend.at[0]
        to_up, to_down, n = rows.at[g, 6 + i], rows.at[g, 2 + i], p + 8 if h else p
        if h is not None:
            src, to_up, to_down = (ref.at[:, halves[h]] for ref in (src, to_up, to_down))
        near_in.setdefault((p, 3), []).append(remote(src, to_up, a_r.at[1, n], up))
        near_in.setdefault((p, 1), []).append(remote(src, to_down, a_r.at[0, n], down))

    pick = pick[:, :32].astype(BF)
    step = 1024
    for h, at in enumerate(halves):
        landed(xtok.at[pl.ds(1, 3), :, at], x_r.at[h])
        for n in range(h * half, h * half + half, step):
            piece = jnp.dot(pick, xtok[:, :, n : n + step].reshape(32, step), preferred_element_type=F32).astype(BF)
            zsend[0, :, n : n + step] = piece[:16]
            zsend[1, :, n : n + step] = piece[16:]
            rows[0, 0, :, n : n + step] = piece[:16]
        send_z(1, zsend.at[1, :, at], 1 + 8 * h, -1, at)
        send_z(7, zsend.at[1, :, at], 7 + 3 * h, 1, at)
        send_y(0, h)
    send_z(2, zsend.at[0], 2, -2)
    send_z(6, zsend.at[0], 6, 2)

    def pass_z(dz):
        g, i = PLACE[dz]
        hop = -2 if dz < 4 else 2
        if dz in (1, 7):
            send_z((dz - hop) % NZ, rows.at[g, i], (dz - hop) % NZ, hop)
        if dz in (2, 6):
            at = halves[dz // 4]
            send_z(4, rows.at[g, i, :, at], {2: 4, 6: 8}[dz], hop, at)

    def spread_own(p):
        dz = ORDER[p]
        for copy in z_in[dz]:
            copy.wait_recv()
        pass_z(dz)
        send_y(p)

    def spread_first():
        for h in range(2):
            for p in (1, 2):
                z_in[ORDER[p]][h].wait_recv()
                send_y(p, h)
                if h:
                    pass_z(ORDER[p])

    def spread_on(p):
        g, i = divmod(p, 2)
        came, to, ry = (3, up, 6) if i == 0 else (1, down, 3)
        for copy in near_in[p, came]:
            copy.wait_recv()
        remote(rows.at[g, ry], rows.at[g, 4 + i], d_r.at[g], to)

    def arrived(g):
        for p, ry in ((2 * g, 1), (2 * g + 1, 3)):
            for copy in near_in[p, ry]:
                copy.wait_recv()
        landed(rows.at[g, pl.ds(4, 2)], d_r.at[g])

    def ffn_up(g):
        for n in range(0, 2 * own_hidden, 256):
            at = pl.ds(n, 256)
            block = rows[g].reshape(128, width)
            gate = jnp.dot(block, wg[:, at], preferred_element_type=F32)
            upward = jnp.dot(block, wu[:, at], preferred_element_type=F32)
            hid[:, at] = (gate / (1.0 + jnp.exp(-gate)) * upward).astype(BF)

    def ffn_down(g):
        @pl.loop(0, width // DOWN)
        def _(n):
            at = pl.ds(pl.multiple_of(n * DOWN, DOWN), DOWN)
            out = jnp.dot(hid[...], wd[:, at], preferred_element_type=F32)
            part[g, :, :, at] = out.astype(BF).reshape(8, 16, DOWN)

    relay_in = {}

    def final(g, side, i, h):
        src = part.at[g, ((2, 3), (6, 7))[side][i], :, halves[h]]
        dst = fin.at[side, g - 2, i, :, halves[h]]
        at = 2 * (g - 2) + i
        remote(src, dst, c_r.at[at, h], (up, down)[side])

    def reduce_first(g):
        for h in range(2):
            for side in range(2):
                src, dst = part.at[g, 4 + side, :, halves[h]], fwd.at[side, g - 2, :, halves[h]]
                relay_in[g, side, h] = remote(src, dst, f_r.at[side, g - 2, h], (up, down)[side])
        for h in range(2):
            final(g, 0, 1, h)
            final(g, 1, 0, h)

    def reduce_on(g):
        for h in range(2):
            for side, ry in ((0, 2), (1, 7)):
                relay_in[g, side, h].wait_recv()
                for n in range(h * half, h * half + half, step):
                    at = slice(n, n + step)
                    part[g, ry, :, at] = (part[g, ry, :, at].astype(F32) + fwd[side, g - 2, :, at].astype(F32)).astype(BF)
                final(g, side, side, h)

    row = lax.broadcasted_iota(jnp.int32, (32, 96), 0)
    col = lax.broadcasted_iota(jnp.int32, (32, 96), 1)
    fold = jnp.where(((row // 4) % 2 == col // 48) & (row // 8 * 4 + row % 4 == col % 16), 1.0, 0.0).astype(BF)

    def finish(g):
        for h in range(2):
            for i in (1, 0):
                landed(fin.at[:, g - 2, i, :, halves[h]], c_r.at[2 * (g - 2) + i, h])
                dz = ORDER[2 * g + i]
                slot = SUMMED.index(NZ - dz)
                terms = [
                    ref[:, m : m + step]
                    for m in (h * half, h * half + step)
                    for ref in (part.at[g, i], fin.at[0, g - 2, i], fin.at[1, g - 2, i])
                ]
                total = jnp.dot(fold, jnp.concatenate(terms, axis=0), preferred_element_type=F32).astype(BF)
                at = pl.ds(h * step, step)
                for k in range(NX):
                    zsum[g - 2, i, k, :, h * step : h * step + step] = total[8 * k : 8 * k + 8]
                for k in (2, 1, 3, 0):
                    to = (NX - k) % NX
                    remote(zsum.at[g - 2, i, k, :, at], ret.at[slot, to, :, at], b_r.at[0], device(k, 0, dz), all_s.at[3])

    row = lax.broadcasted_iota(jnp.int32, (32, 32), 0)
    col = lax.broadcasted_iota(jnp.int32, (32, 32), 1)
    fold_one = jnp.where(((row // 4) % 2 == col // 16) & (row // 8 * 4 + row % 4 == col % 16), 1.0, 0.0).astype(BF)

    def go_back(g):
        for i in range(2):
            dz = ORDER[2 * g + i]
            slot = STRAIGHT.index((NZ - dz) % NZ)
            for ry in range(NY):
                for n in range(0, half, step):
                    terms = [part[g, 2 * ry + i, :, 2 * n + m : 2 * n + m + step] for m in (0, step)]
                    moved = jnp.dot(fold_one, jnp.concatenate(terms, axis=0), preferred_element_type=F32).astype(BF)
                    for k in range(NX):
                        if dz or k:
                            zback[g, i, k, ry, :, n : n + step] = moved[8 * k : 8 * k + 8]
                        else:
                            near[0, 0, ry, :, n : n + step] = moved[:8]
            for k in (2, 1, 3, 0):
                to = (NX - k) % NX
                if dz or k:
                    remote(zback.at[g, i, k], near.at[slot, to], n_r.at[min(slot, 1)], device(k, 0, dz), all_s.at[i if g == 0 else 2])

    def token_mix(info, flip):
        row = lax.broadcasted_iota(jnp.int32, (128, 128), 0)
        lane = lax.broadcasted_iota(jnp.int32, (128, 128), 1)
        wanted = (2 * ((x + (row // 8) % 4) % NX) + (z + (row // 32 + 1) // 2 + flip) % 2).astype(F32)
        id0, id1, w0, w1 = (jnp.broadcast_to(info[k : k + 1, :], (128, 128)) for k in range(4))
        first = id0 == wanted
        member = first | (id1 == wanted)
        position = jnp.dot(jnp.where(member, 1.0, 0.0).astype(BF), before, preferred_element_type=F32)
        chosen = member & (position == (row % 4).astype(F32)) & (lane // 8 == (row // 4) % 2)
        spread = jnp.where(chosen, jnp.where(first, w0, w1), 0.0).T
        coarse = spread.astype(BF)
        fine = (spread - coarse.astype(F32)).astype(BF)
        return jnp.concatenate([coarse[:16], fine[:16]], axis=0)

    def sum_straight():
        landed(near.at[0, pl.ds(1, 3)], n_r.at[0])
        landed(near.at[pl.ds(1, 3)], n_r.at[1])
        for ry in (2, 1, 3, 0):
            for n in range(0, half, step):
                both = jnp.dot(ymix[ry], near[:, :, ry, :, n : n + step].reshape(128, step), preferred_element_type=F32)
                total = both[:16] + both[16:]
                for m in range(2):
                    at = slice(2 * n + m * step, 2 * n + m * step + step)
                    if ry:
                        ysum[ry - 1, :, at] = total[8 * m : 8 * m + 8].astype(BF)
                    else:
                        yown[:, at] = total[8 * m : 8 * m + 8]
            if ry:
                remote(ysum.at[ry - 1], yret.at[NY - ry - 1], y_r.at[0], device(0, ry, 0), all_s.at[4])

    weight_parts(3)
    mix[...] = token_mix(xinfo[0], 1)
    spread_first()
    weight_parts(3)
    spread_on(0)
    spread_on(1)
    spread_own(3)
    spread_own(6)
    for load in loads:
        load.wait()
    arrived(0)
    for n, ref in enumerate((wg.at[:, far], wu.at[:, far], wd.at[far])):
        landed(ref, w_r.at[n])
    ffn_up(0)
    spread_on(2)
    spread_own(4)
    ffn_down(0)
    spread_on(3)
    go_back(0)
    spread_own(5)
    spread_own(7)
    arrived(1)
    ffn_up(1)
    spread_on(4)
    spread_on(6)
    spread_on(5)
    ffn_down(1)
    go_back(1)
    spread_on(7)
    landed(yinfo.at[pl.ds(1, 3)], j_r.at[0])
    ymix[0] = token_mix(xinfo[0], 0)
    for k in range(1, NY):
        ymix[k] = token_mix(yinfo[k], 0)
    arrived(2)
    ffn_up(2)
    ffn_down(2)
    reduce_first(2)
    arrived(3)
    ffn_up(3)
    ffn_down(3)
    reduce_on(2)
    reduce_first(3)
    finish(2)
    reduce_on(3)
    finish(3)
    sum_straight()

    landed(yret, y_r.at[0])
    landed(ret, b_r.at[0])
    for n in range(0, half, step):
        both = jnp.dot(mix[...], ret[:, :, :, n : n + step].reshape(128, step), preferred_element_type=F32)
        total = both[:16] + both[16:]
        for m in range(2):
            at = slice(2 * n + m * step, 2 * n + m * step + step)
            rest = yown[:, at]
            for k in range(NY - 1):
                rest = rest + yret[k, :, at].astype(F32)
            out_ref[:, at] = (total[8 * m : 8 * m + 8] + rest).astype(BF)
    for copy in sent[-POOL:]:
        copy.wait_send()
    for n, ref in enumerate((zback.at[0, 0, pl.ds(1, 3)], zback.at[0, 1], zback.at[1], zsum, ysum)):
        landed(ref, all_s.at[n])


def shards(tokens, expert_ids, route_weights, w_gate, w_up, w_down):
    block, width = tokens.shape
    hidden = w_gate.shape[2]
    dma = pltpu.SemaphoreType.DMA
    vmem = pl.BlockSpec(memory_space=pltpu.VMEM)
    hbm = pl.BlockSpec(memory_space=pl.ANY)
    return pl.pallas_call(
        kernel,
        out_shape=jax.ShapeDtypeStruct((block, width), BF),
        in_specs=[hbm] * 6,
        out_specs=vmem,
        scratch_shapes=[
            pltpu.VMEM((NX, block, width), BF),
            pltpu.VMEM((NX, 8, 128), F32),
            pltpu.VMEM((2, 16, width), BF),
            pltpu.VMEM((GROUPS, 8, 16, width), BF),
            pltpu.VMEM((width, 2 * hidden), BF),
            pltpu.VMEM((width, 2 * hidden), BF),
            pltpu.VMEM((2 * hidden, width), BF),
            pltpu.VMEM((128, 2 * hidden), BF),
            pltpu.VMEM((GROUPS, 8, 16, width), BF),
            pltpu.VMEM((2, 2, 16, width), BF),
            pltpu.VMEM((2, 2, 2, 16, width), BF),
            pltpu.VMEM((2, 2, NX, 8, width // 2), BF),
            pltpu.VMEM((4, NX, 8, width // 2), BF),
            pltpu.VMEM((32, 128), BF),
            pltpu.VMEM((NY, 8, 128), F32),
            pltpu.VMEM((2, 2, NX, NY, 8, width // 2), BF),
            pltpu.VMEM((4, NX, NY, 8, width // 2), BF),
            pltpu.VMEM((NY, 32, 128), BF),
            pltpu.VMEM((3, block, width), BF),
            pltpu.VMEM((block, width), F32),
            pltpu.VMEM((3, block, width), BF),
            pltpu.VMEM((2, 8), jnp.int32),
            pltpu.VMEM((2, 8), F32),
            dma((POOL,)), dma((5,)),
            dma((2,)), dma((1,)),
            dma((11,)),
            dma((2, 11)), dma((4,)),
            dma((2, 2, 2)), dma((4, 2)),
            dma((1,)),
            dma((2,)),
            dma((1,)), dma((1,)),
            dma((3,)),
            dma((3,)), dma((3,)),
        ],
        compiler_params=pltpu.CompilerParams(
            collective_id=0, has_side_effects=True, vmem_limit_bytes=62 * 1024 * 1024
        ),
    )(tokens, expert_ids.T, route_weights.T, w_gate, w_up, w_down)


def solution(mesh):
    placed = (
        P(("expert", "shard"), None),
        P(("expert", "shard"), None),
        P(("expert", "shard"), None),
        P("expert", None, "shard"),
        P("expert", None, "shard"),
        P("expert", "shard", None),
    )
    return jax.shard_map(
        shards, mesh=mesh, in_specs=placed, out_specs=P(("expert", "shard"), None), check_vma=False
    )
```

time: 88.1 us -> 84.9 us (0.964); the launches traced: 87.9 us -> 83.7 us
  Pallas kernels: 86.4 us -> 82.3 us
    pallas_call x1, Pallas kernels: 86.4 us -> 82.3 us  [shards(): pl.pallas_call(kernel, out_shape=jax.ShapeDtypeStruct((block, width), BF)...]
where the time goes in v4:
time: 84.9 us; the launch traced here: 83.7 us
  Pallas kernels  82.3 us (97%)
  local copies, waits for them, and re-layouts  1.47 us (2%)
    pallas_call x1, Pallas kernels, shards(): pl.pallas_call(kernel, out_shape=jax.ShapeDtypeStruct((block, width), BF)...  82.3 us

profile of v4, /device:TPU:24, one launch (start us, length us, event | category | flops | bytes accessed | tf_op | source)
XLA Modules:
  0.0 83.7 jit_solution(4443286910982763365)
XLA Ops:
  0.0 82.3 %shard_map.64 = bf16[8,4096]{1,0:T(8,128)(2,1)} custom-call(bf16[8,4096]{1,0:T(8,128)(2,1)} %tok_ref.1, s32[2,8]{1,0:T(2,128)} %bitcast.2, f32[2,8]{1,0:T(2,128)} %bitcast.3, bf16[1,4096,384]{2,1,0:T(8,128)(2,1)} %wg_ref.1, bf16[1,4096,384]{2,1,0:T(8,128)(2,1)} %wu_ref.1, bf16[1,384,4096]{2,1,0:T(8,128)(2,1)} %wd_ref.1), custom_call_target="tpu_custom_call" | custom-call | tf_op jit(solution)/shard_map/pallas_call | solution.py:394
  82.3 1.5 %copy.8 = bf16[8,4096]{1,0:T(8,128)(2,1)} copy(bf16[8,4096]{1,0:T(8,128)(2,1)} %shard_map.64) | data formatting | bytes 131072

commit v5 on v4

--- a/solution.py
+++ b/solution.py
@@ -15,7 +15,7 @@
 STRAIGHT = (0, 7, 1, 6)
 SUMMED = (3, 4, 2, 5)
 PARTS = 4
-POOL = 40
+POOL = 32
 DOWN = 2048
 
 
@@ -228,11 +228,15 @@
         at = 2 * (g - 2) + i
         remote(src, dst, c_r.at[at, h], (up, down)[side])
 
-    def reduce_first(g):
+    def down_and_reduce(g):
         for h in range(2):
+            out = jnp.dot(hid[...], wd[:, halves[h]], preferred_element_type=F32)
+            part[g, :, :, halves[h]] = out.astype(BF).reshape(8, 16, half)
             for side in range(2):
                 src, dst = part.at[g, 4 + side, :, halves[h]], fwd.at[side, g - 2, :, halves[h]]
                 relay_in[g, side, h] = remote(src, dst, f_r.at[side, g - 2, h], (up, down)[side])
+
+    def reduce_first(g):
         for h in range(2):
             final(g, 0, 1, h)
             final(g, 1, 0, h)
@@ -356,11 +360,11 @@
         ymix[k] = token_mix(yinfo[k], 0)
     arrived(2)
     ffn_up(2)
-    ffn_down(2)
+    down_and_reduce(2)
     reduce_first(2)
     arrived(3)
     ffn_up(3)
-    ffn_down(3)
+    down_and_reduce(3)
     reduce_on(2)
     reduce_first(3)
     finish(2)
@@ -393,7 +397,7 @@
     hbm = pl.BlockSpec(memory_space=pl.ANY)
     return pl.pallas_call(
         kernel,
-        out_shape=jax.ShapeDtypeStruct((block, width), BF),
+        out_shape=pltpu.VMEM((block, width), BF),
         in_specs=[hbm] * 6,
         out_specs=vmem,
         scratch_shapes=[

time: 84.9 us -> 82.9 us (0.976)
  no operation moved by 1% of the time
where the time goes in v5:
time: 82.9 us; the launch traced here: 82.2 us
  Pallas kernels  81.6 us (98%)
    pallas_call x1, Pallas kernels, shards(): pl.pallas_call(kernel, out_shape=pltpu.VMEM((block, width), BF), in_specs...  81.6 us

profile of v5, /device:TPU:24, one launch (start us, length us, event | category | flops | bytes accessed | tf_op | source)
XLA Modules:
  0.0 82.2 jit_solution(7110777017121522504)
XLA Ops:
  0.0 81.6 %shard_map.64 = bf16[8,4096]{1,0:T(8,128)(2,1)S(1)} custom-call(bf16[8,4096]{1,0:T(8,128)(2,1)} %tok_ref.1, s32[2,8]{1,0:T(2,128)} %bitcast.2, f32[2,8]{1,0:T(2,128)} %bitcast.3, bf16[1,4096,384]{2,1,0:T(8,128)(2,1)} %wg_ref.1, bf16[1,4096,384]{2,1,0:T(8,128)(2,1)} %wu_ref.1, bf16[1,384,4096]{2,1,0:T(8,128)(2,1)} %wd_ref.1), custom_call_target="tpu_custom_call" | custom-call | tf_op jit(solution)/shard_map/pallas_call | solution.py:398
  81.6 0.6 copy.8
